TPU v7x, 32 devices: a whole 2x2x4 slice. The times are simulated.
32 devices in a mesh: layer: 8 (over y, x, core), dp: 4 (over z).
Axes of the slice: x: 2, y: 2, z: 4, core: 2. Of those that a mesh axis runs over, the one named last changes fastest.
Arguments:
- initial: float32 [256, 1024], P('dp'), may hold values from -6 to 6
- norm_gains: float32 [32, 1024], P('layer'), may hold values from 0.25 to 1.75
- first_weights: bfloat16 [32, 1024, 2048], P('layer'), may hold values from -0.1875 to 0.1875
- second_weights: bfloat16 [32, 2048, 1024], P('layer'), may hold values from -0.046875 to 0.046875
Outputs:
- layer_states: float32 [32, 256, 1024], P('layer', 'dp')
- residual_ratios: float32 [7], replicated
- coarse_defects_four: float32 [32, 256, 1024], P('layer', 'dp')
- coarse_defects_sixteen: float32 [32, 256, 1024], P('layer', 'dp')
All inputs are finite; a program needn't handle non-finite values.
Results may differ from a plain program's by a relative error of at most 0.02.
Values sent between devices are 32-bit elements; how exact they have to be, the bound alone decides.
A program may use at most 128 MiB of HBM per device.

v0:
```python
import jax
import jax.numpy as jnp
from jax import lax
from jax.sharding import PartitionSpec as P

epsilon = 1e-06


def shifted(block, axis, distance):
    devices = range(lax.axis_size(axis))
    route = [(i - distance, i) for i in devices if i - distance in devices]
    return lax.ppermute(block, axis, route)


def branch(row_block, weight_in, weight_out, gain_row):
    mean_square = jnp.mean(row_block * row_block, axis=-1, keepdims=True)
    normed = (row_block * lax.rsqrt(mean_square + epsilon) * gain_row).astype(jnp.bfloat16)
    hidden = jax.nn.gelu(
        jnp.dot(normed, weight_in, preferred_element_type=jnp.float32), approximate=True
    ).astype(jnp.bfloat16)
    return jnp.dot(hidden, weight_out, preferred_element_type=jnp.float32)


def local(initial, norm_gains, first_weights, second_weights):
    slot_count = first_weights.shape[0]
    sections = lax.axis_size("layer")
    layer_total = slot_count * sections
    norm_count = layer_total // 4 - 1
    first_point = lax.axis_index("layer") * slot_count
    points = first_point + jnp.arange(slot_count, dtype=jnp.int32) + 1
    spacings = (1, 4, 16)

    def shaped(flags, rank):
        return flags.reshape((slot_count,) + (1,) * (rank - 1))

    def previous(values, level_index):
        spacing = spacings[level_index]
        if spacing >= slot_count:
            portion = values
            distance = spacing // slot_count
        else:
            portion = values[slot_count - spacing :]
            distance = 1
        if level_index == 0:
            arrived = shifted(portion, "layer", distance)
        elif level_index == 1:
            arrived = shifted(portion, "layer", distance)
        else:
            arrived = shifted(portion, "layer", distance)
        if spacing < slot_count:
            arrived = jnp.concatenate([arrived, values[: slot_count - spacing]], axis=0)
        return arrived

    def incoming(values, level_index, anchor):
        arrived = previous(values, level_index)
        from_anchor = shaped(points - spacings[level_index] == 0, values.ndim)
        return jnp.where(from_anchor, anchor, arrived)

    def advance(before, level_index, active, right_side):
        factor = float(spacings[level_index])
        results = []
        for slot in range(slot_count):

            def advance_compute(values, source, slot=slot):
                return (
                    values
                    + factor
                    * branch(values, first_weights[slot], second_weights[slot], norm_gains[slot])
                    + source
                )

            def advance_unchanged(values, source):
                return values

            source = right_side[slot] if right_side is not None else jnp.zeros_like(before[slot])
            results.append(
                lax.cond(active[slot], advance_compute, advance_unchanged, before[slot], source)
            )
        return jnp.stack(results)

    def relaxation(current, level_index, residues, right_side, anchor):
        modulus = 4 * spacings[level_index]
        for residue in residues:
            before = incoming(current, level_index, anchor)
            active = points % modulus == residue
            current = jnp.where(
                shaped(active, 3), advance(before, level_index, active, right_side), current
            )
        return (current, None)

    def restrict(current, level_index, right_side, anchor):
        spacing = spacings[level_index]
        factor = float(spacing)
        wide_factor = float(4 * spacing)
        before = incoming(current, level_index, anchor)
        far_state = incoming(current, level_index + 1, anchor)
        active = points % (4 * spacing) == 0
        row_count = current.shape[1]
        coarse_list = []
        gap_list = []
        step_list = []
        for slot in range(slot_count):

            def restrict_compute(near, distant, held, source, slot=slot):
                update = branch(
                    jnp.concatenate([near, distant], axis=0),
                    first_weights[slot],
                    second_weights[slot],
                    norm_gains[slot],
                )
                near_term = update[:row_count]
                fine_value = near + factor * near_term + source
                coarse = fine_value - (distant + wide_factor * update[row_count:])
                gap = fine_value - held
                return (coarse, jnp.sum(gap * gap), jnp.sum(near_term * near_term))

            def restrict_unchanged(near, distant, held, source):
                nothing = jnp.zeros((), near.dtype)
                return (jnp.zeros_like(near), nothing, nothing)

            source = right_side[slot] if right_side is not None else jnp.zeros_like(before[slot])
            coarse, gap_sum, step_sum = lax.cond(
                active[slot],
                restrict_compute,
                restrict_unchanged,
                before[slot],
                far_state[slot],
                current[slot],
                source,
            )
            coarse_list.append(coarse)
            gap_list.append(gap_sum)
            step_list.append(step_sum)
        return (jnp.stack(coarse_list), jnp.stack(gap_list), jnp.stack(step_list))

    def defects(current, level_index, anchor):
        spacing = spacings[level_index]
        factor = float(spacing)
        before = incoming(current, level_index, anchor)
        stepped = []
        for slot in range(slot_count):
            stepped.append(
                before[slot]
                + factor
                * branch(before[slot], first_weights[slot], second_weights[slot], norm_gains[slot])
            )
        valid = shaped(points >= spacing, 3)
        return jnp.where(valid, current - jnp.stack(stepped), 0.0)

    def multigrid_cycle(anchor):
        current = jnp.broadcast_to(anchor, (slot_count,) + anchor.shape)
        current, unused = relaxation(current, 0, (1, 2, 3), None, anchor)
        current, unused = relaxation(current, 0, (0,), None, anchor)
        current, carried = relaxation(current, 0, (1, 2, 3), None, anchor)
        rhs_one, gap_sums, step_sums = restrict(current, 0, None, anchor)
        current, carried = relaxation(current, 1, (4, 8, 12), rhs_one, anchor)
        rhs_two, unused_gaps, unused_steps = restrict(current, 1, rhs_one, anchor)
        for coarse_step in range(1, layer_total // 16 + 1):
            active = points == 16 * coarse_step
            before = incoming(current, 2, anchor)
            current = jnp.where(shaped(active, 3), advance(before, 2, active, rhs_two), current)
        current, unused = relaxation(current, 1, (4, 8, 12), rhs_one, anchor)
        current, unused = relaxation(current, 0, (1, 2, 3), None, anchor)
        defects_four = defects(current, 1, anchor)
        defects_sixteen = defects(current, 2, anchor)
        return (current, gap_sums, step_sums, defects_four, defects_sixteen)

    portions = [initial]
    outcomes = [multigrid_cycle(portion) for portion in portions]
    layer_states = jnp.concatenate([outcome[0] for outcome in outcomes], axis=1)
    defects_four = jnp.concatenate([outcome[3] for outcome in outcomes], axis=1)
    defects_sixteen = jnp.concatenate([outcome[4] for outcome in outcomes], axis=1)
    gap_sums = outcomes[0][1]
    step_sums = outcomes[0][2]
    counted = (points % 4 == 0) & (points >= 8)
    entry_index = points // 4 - 2
    one_hot = (
        (jnp.arange(norm_count, dtype=jnp.int32)[None, :] == entry_index[:, None])
        & counted[:, None]
    ).astype(jnp.float32)
    gap_vector = jnp.sum(gap_sums[:, None] * one_hot, axis=0)
    step_vector = jnp.sum(step_sums[:, None] * one_hot, axis=0)
    gap_total, step_total = lax.psum((gap_vector, step_vector), ("layer", "dp"))
    residual_ratios = jnp.sqrt(gap_total / (step_total + epsilon))
    return (layer_states, residual_ratios, defects_four, defects_sixteen)


def local_quads(initial, norm_gains, first_weights, second_weights):
    sections = lax.axis_size("layer")
    blocks = sections // 4
    here = lax.axis_index("layer")
    place = here % 4
    rows = initial.shape[0]

    def moved(slot, *states):
        stacked = states[0] if len(states) == 1 else jnp.concatenate(states, axis=0)
        return branch(stacked, first_weights[slot], second_weights[slot], norm_gains[slot])

    def near(values):
        return jnp.where(here == 0, initial, shifted(values, "layer", 1))

    def distant(values):
        return jnp.where(here == 3, initial, shifted(values, "layer", 4))

    state = initial
    for slot in range(4):
        state = state + moved(slot, state)
    point = state
    left = near(point)
    far = distant(point)
    state = left
    for slot in range(3):
        state = state + moved(slot, state)
    update = moved(3, state, left, far)
    near_term = update[:rows]
    fine = state + near_term
    rhs_one = fine - (left + 4.0 * update[rows : 2 * rows])
    far_step = far + 16.0 * update[2 * rows :]
    gap = fine - point
    gap_sum = jnp.sum(gap * gap)
    step_sum = jnp.sum(near_term * near_term)
    point = jnp.where(place == 0, fine, point)
    for residue in (1, 2, 3):
        before = near(point)
        stepped = before + 4.0 * moved(3, before) + rhs_one
        point = jnp.where(place == residue, stepped, point)
    rhs_two = point - far_step
    wide = place == 3
    factor = jnp.where(wide, 16.0, 4.0)
    source = jnp.where(wide, rhs_two, rhs_one)
    for block in range(1, blocks):
        before = jnp.where(wide, distant(point), near(point))
        stepped = before + factor * moved(3, before) + source
        point = jnp.where((here == 4 * block) | (here == 4 * block + 3), stepped, point)
    for residue in (1, 2):
        before = near(point)
        stepped = before + 4.0 * moved(3, before) + rhs_one
        point = jnp.where(place == residue, stepped, point)
    left = near(point)
    far = distant(point)
    state = left
    states = []
    for slot in range(3):
        state = state + moved(slot, state)
        states.append(state)
    states.append(point)
    lefts = [shifted(s, "layer", 1) for s in states[:3]] + [left]
    fars = [shifted(s, "layer", 4) for s in states[:3]] + [far]
    fours = []
    sixteens = []
    for slot in range(4):
        update = moved(slot, lefts[slot], fars[slot])
        fours.append(states[slot] - (lefts[slot] + 4.0 * update[:rows]))
        sixteens.append(states[slot] - (fars[slot] + 16.0 * update[rows:]))
    points = here * 4 + jnp.arange(4, dtype=jnp.int32) + 1
    defects_four = jnp.where((points >= 4)[:, None, None], jnp.stack(fours), 0.0)
    defects_sixteen = jnp.where((points >= 16)[:, None, None], jnp.stack(sixteens), 0.0)
    one_hot = (jnp.arange(sections - 1) == here - 1).astype(jnp.float32)
    gap_total, step_total = lax.psum((gap_sum * one_hot, step_sum * one_hot), ("layer", "dp"))
    ratios = jnp.sqrt(gap_total / (step_total + epsilon))
    return (jnp.stack(states), ratios, defects_four, defects_sixteen)


def chosen(initial, norm_gains, first_weights, second_weights):
    quads = first_weights.shape[0] == 4 and lax.axis_size("layer") % 4 == 0
    return (local_quads if quads else local)(initial, norm_gains, first_weights, second_weights)


def solution(mesh):
    placed = (P("dp", None), P("layer", None), P("layer", None, None), P("layer", None, None))
    return jax.shard_map(
        chosen,
        mesh=mesh,
        in_specs=placed,
        out_specs=(P("layer", "dp", None), P(), P("layer", "dp", None), P("layer", "dp", None)),
        check_vma=False,
    )
```

profile of v0, /device:TPU:0, one launch (start us, length us, event | category | flops | bytes accessed | tf_op | source)
XLA Modules:
  0.0 269.5 jit_solution(11445225732891216298)
XLA Ops:
  0.6 1.1 multiply_reduce_fusion.22
  1.7 0.9 fusion.815
  2.6 5.4 %multiply_reduce_fusion.21 = (f32[64]{0:T(128)S(1)}, f32[64,1024]{1,0:T(8,128)S(1)}) fusion(f32[64,1024]{1,0:T(8,128)} %param.4, bf16[4,2048,1024]{2,1,0:T(8,128)(2,1)} %param.7, bf16[4,1024,2048]{2,1,0:T(8,128)(2,1)} %param.6, f32[1024]{0:T(1024)S(1)} %bitcast.351, f32[64]{0:T(128)S(1)} %add_rsqrt_fusion.20), kind=kOutput, calls=%fused_computation.443 | convolution fusion | flops 538443712 | bytes 9179648 | tf_op jit(solution)/shard_map/dot_general | solution.py:21
  8.0 5.4 %multiply_reduce_fusion.20 = (f32[64]{0:T(128)S(1)}, f32[64,1024]{1,0:T(8,128)S(1)}) fusion(f32[64,1024]{1,0:T(8,128)S(1)} %get-tuple-element.33, bf16[4,2048,1024]{2,1,0:T(8,128)(2,1)} %param.7, bf16[4,1024,2048]{2,1,0:T(8,128)(2,1)} %param.6, f32[1024]{0:T(1024)S(1)} %bitcast.338, f32[64]{0:T(128)S(1)} %add_rsqrt_fusion.19), kind=kOutput, calls=%fused_computation.441 | convolution fusion | flops 538443712 | bytes 9179904 | tf_op jit(solution)/shard_map/dot_general | solution.py:21
  13.4 5.3 %multiply_reduce_fusion.19 = (f32[64]{0:T(128)S(1)}, f32[64,1024]{1,0:T(8,128)S(1)}) fusion(f32[64,1024]{1,0:T(8,128)S(1)} %get-tuple-element.35, bf16[4,2048,1024]{2,1,0:T(8,128)(2,1)} %param.7, bf16[4,1024,2048]{2,1,0:T(8,128)(2,1)} %param.6, f32[1024]{0:T(1024)S(1)} %bitcast.334, f32[64]{0:T(128)S(1)} %add_rsqrt_fusion.18), kind=kOutput, calls=%fused_computation.439 | convolution fusion | flops 538443712 | bytes 9179904 | tf_op jit(solution)/shard_map/dot_general | solution.py:21
  18.8 5.2 %fusion.120 = f32[64,1024]{1,0:T(8,128)S(1)} fusion(f32[64,1024]{1,0:T(8,128)S(1)} %get-tuple-element.37, bf16[4,2048,1024]{2,1,0:T(8,128)(2,1)} %param.7, bf16[4,1024,2048]{2,1,0:T(8,128)(2,1)} %param.6, f32[1024]{0:T(1024)S(1)} %bitcast.342, f32[64]{0:T(128)S(1)} %add_rsqrt_fusion.17), kind=kOutput, calls=%fused_computation.121 | convolution fusion | flops 538312704 | bytes 9179648 | tf_op jit(solution)/shard_map/dot_general | solution.py:21
  24.0 4.9 %collective-permute-start.1 = (f32[64,1024]{1,0:T(8,128)S(1)}, f32[64,1024]{1,0:T(8,128)S(1)}, u32[]{:S(2)}, u32[]{:S(2)}) collective-permute-start(f32[64,1024]{1,0:T(8,128)S(1)} %fusion.120), channel_id=1, source_target_pairs={{0,16},{4,20},{8,24},{12,28},{1,17},{5,21},{9,25},{13,29},{2,18},{... | collective-permute-start | bytes 786440 | tf_op jit(solution)/shard_map/ppermute | solution.py:12
  28.9 1.7 collective-permute-start
  30.6 6.7 %collective-permute-done.1 = f32[64,1024]{1,0:T(8,128)S(1)} collective-permute-done((f32[64,1024]{1,0:T(8,128)S(1)}, f32[64,1024]{1,0:T(8,128)S(1)}, u32[]{:S(2)}, u32[]{:S(2)}) %collective-permute-start.1) | collective-permute-done | bytes 262176 | tf_op jit(solution)/shard_map/ppermute | solution.py:12
  37.2 0.1 multiply_reduce_fusion.18
  37.4 5.3 %multiply_reduce_fusion.17 = (f32[64]{0:T(128)S(1)}, f32[64,1024]{1,0:T(8,128)S(1)}) fusion(f32[64,1024]{1,0:T(8,128)S(1)} %get-tuple-element.13, bf16[4,2048,1024]{2,1,0:T(8,128)(2,1)} %param.7, bf16[4,1024,2048]{2,1,0:T(8,128)(2,1)} %param.6, f32[64]{0:T(128)S(1)} %add_rsqrt_fusion.16, f32[1024]{0:T(1024)S(1)} %bitcast.352), kind=kOutput, calls=%fused_computation.435 | convolution fusion | flops 538443712 | bytes 9179904 | tf_op jit(solution)/shard_map/dot_general | solution.py:21
  42.7 5.3 %multiply_reduce_fusion.16 = (f32[64]{0:T(128)S(1)}, f32[64,1024]{1,0:T(8,128)S(1)}) fusion(f32[64,1024]{1,0:T(8,128)S(1)} %get-tuple-element.39, bf16[4,2048,1024]{2,1,0:T(8,128)(2,1)} %param.7, bf16[4,1024,2048]{2,1,0:T(8,128)(2,1)} %param.6, f32[64]{0:T(128)S(1)} %add_rsqrt_fusion.15, f32[1024]{0:T(1024)S(1)} %bitcast.339), kind=kOutput, calls=%fused_computation.433 | convolution fusion | flops 538443712 | bytes 9179904 | tf_op jit(solution)/shard_map/dot_general | solution.py:21
  48.1 5.2 %fusion.216 = f32[64,1024]{1,0:T(8,128)S(1)} fusion(f32[64,1024]{1,0:T(8,128)S(1)} %get-tuple-element.41, bf16[4,2048,1024]{2,1,0:T(8,128)(2,1)} %param.7, bf16[4,1024,2048]{2,1,0:T(8,128)(2,1)} %param.6, f32[64]{0:T(128)S(1)} %add_rsqrt_fusion.14, f32[1024]{0:T(1024)S(1)} %bitcast.335), kind=kOutput, calls=%fused_computation.153 | convolution fusion | flops 538312704 | bytes 9179648 | tf_op jit(solution)/shard_map/dot_general | solution.py:21
  53.3 0.1 multiply_reduce_fusion
  53.5 5.7 %fusion.14 = f32[192,1024]{1,0:T(8,128)S(1)} fusion(f32[64,1024]{1,0:T(8,128)S(1)} %get-tuple-element.27, f32[64,1024]{1,0:T(8,128)S(1)} %get-tuple-element.13, f32[64,1024]{1,0:T(8,128)S(1)} %fusion.216, f32[1024]{0:T(1024)S(1)} %bitcast.343, f32[192]{0:T(256)S(1)} %add_rsqrt_fusion, bf16[4,2048,1024]{2,1,0:T(8,128)(2,1)} %param.7, ...), kind=kOutput, calls=%fused_computation.14 | convolution fusion | flops 1615134720 | bytes 9966336 | tf_op jit(solution)/shard_map/dot_general | solution.py:21
  59.2 0.7 multiply_reduce_fusion.5
  59.9 1.3 collective-permute-start.2
  61.2 1.1 collective-permute-done.2
  62.4 5.2 %fusion.192 = f32[64,1024]{1,0:T(8,128)S(1)} fusion(f32[64,1024]{1,0:T(8,128)S(1)} %get-tuple-element.14, f32[64,1024]{1,0:T(8,128)S(1)} %get-tuple-element.15, bf16[4,2048,1024]{2,1,0:T(8,128)(2,1)} %param.7, bf16[4,1024,2048]{2,1,0:T(8,128)(2,1)} %param.6, f32[64]{0:T(128)S(1)} %add_rsqrt_fusion.13, f32[1024]{0:T(1024)S(1)} %bitcast.344, pred[]{:T(512)S(6)} %eq.46, ...), kind=kOutput, calls=%fused_computation.145 | convolution fusion | flops 538640384 | bytes 10229760 | tf_op jit(solution)/shard_map/dot_general | solution.py:21
  67.7 5.6 %collective-permute-start.3 = (f32[64,1024]{1,0:T(8,128)S(1)}, f32[64,1024]{1,0:T(8,128)S(1)}, u32[]{:S(2)}, u32[]{:S(2)}) collective-permute-start(f32[64,1024]{1,0:T(8,128)S(1)} %fusion.192), channel_id=1, source_target_pairs={{0,4},{4,8},{8,12},{12,16},{16,20},{20,24},{24,28},{1,5},{5,9},{9,... | collective-permute-start | bytes 786440 | tf_op jit(solution)/shard_map/ppermute | solution.py:12
  73.3 1.1 collective-permute-done.3
  74.6 5.2 %fusion.189 = f32[64,1024]{1,0:T(8,128)S(1)} fusion(f32[64,1024]{1,0:T(8,128)S(1)} %fusion.192, f32[64,1024]{1,0:T(8,128)S(1)} %get-tuple-element.15, bf16[4,2048,1024]{2,1,0:T(8,128)(2,1)} %param.7, bf16[4,1024,2048]{2,1,0:T(8,128)(2,1)} %param.6, f32[64]{0:T(128)S(1)} %add_rsqrt_fusion.12, f32[1024]{0:T(1024)S(1)} %bitcast.345, pred[]{:T(512)S(6)} %eq.23, ...), kind=kOutput, calls=%fused_computation.144 | convolution fusion | flops 538640384 | bytes 10229760 | tf_op jit(solution)/shard_map/dot_general | solution.py:21
  79.8 6.6 %collective-permute-start.4 = (f32[64,1024]{1,0:T(8,128)S(1)}, f32[64,1024]{1,0:T(8,128)S(1)}, u32[]{:S(2)}, u32[]{:S(2)}) collective-permute-start(f32[64,1024]{1,0:T(8,128)S(1)} %fusion.189), channel_id=1, source_target_pairs={{0,4},{4,8},{8,12},{12,16},{16,20},{20,24},{24,28},{1,5},{5,9},{9,... | collective-permute-start | bytes 786440 | tf_op jit(solution)/shard_map/ppermute | solution.py:12
  86.4 1.1 collective-permute-done.4
  87.6 5.2 %fusion.186 = f32[64,1024]{1,0:T(8,128)S(1)} fusion(f32[64,1024]{1,0:T(8,128)S(1)} %fusion.189, f32[64,1024]{1,0:T(8,128)S(1)} %get-tuple-element.15, bf16[4,2048,1024]{2,1,0:T(8,128)(2,1)} %param.7, bf16[4,1024,2048]{2,1,0:T(8,128)(2,1)} %param.6, f32[64]{0:T(128)S(1)} %add_rsqrt_fusion.11, f32[1024]{0:T(1024)S(1)} %bitcast.346, pred[]{:T(512)S(6)} %eq.49, ...), kind=kOutput, calls=%fused_computation.143 | convolution fusion | flops 538640384 | bytes 10229760 | tf_op jit(solution)/shard_map/dot_general | solution.py:21
  92.9 6.6 %collective-permute-start.6 = (f32[64,1024]{1,0:T(8,128)S(1)}, f32[64,1024]{1,0:T(8,128)S(1)}, u32[]{:S(2)}, u32[]{:S(2)}) collective-permute-start(f32[64,1024]{1,0:T(8,128)S(1)} %fusion.186), channel_id=1, source_target_pairs={{0,4},{4,8},{8,12},{12,16},{16,20},{20,24},{24,28},{1,5},{5,9},{9,... | collective-permute-start | bytes 786440 | tf_op jit(solution)/shard_map/ppermute | solution.py:12
  99.4 8.8 %collective-permute-start.5 = (f32[64,1024]{1,0:T(8,128)S(1)}, f32[64,1024]{1,0:T(8,128)S(1)}, u32[]{:S(2)}, u32[]{:S(2)}) collective-permute-start(f32[64,1024]{1,0:T(8,128)S(1)} %fusion.186), channel_id=1, source_target_pairs={{0,16},{4,20},{8,24},{12,28},{1,17},{5,21},{9,25},{13,29},{2,18},{... | collective-permute-start | bytes 786440 | tf_op jit(solution)/shard_map/ppermute | solution.py:12
  108.3 4.8 %collective-permute-done.5 = f32[64,1024]{1,0:T(8,128)S(1)} collective-permute-done((f32[64,1024]{1,0:T(8,128)S(1)}, f32[64,1024]{1,0:T(8,128)S(1)}, u32[]{:S(2)}, u32[]{:S(2)}) %collective-permute-start.5) | collective-permute-done | bytes 262176 | tf_op jit(solution)/shard_map/ppermute | solution.py:12
  113.1 0.1 multiply_reduce_fusion.12
  113.3 5.3 %fusion.183 = f32[64,1024]{1,0:T(8,128)S(1)} fusion(f32[64,1024]{1,0:T(8,128)S(1)} %fusion.186, f32[64,1024]{1,0:T(8,128)S(1)} %get-tuple-element.11, f32[64,1024]{1,0:T(8,128)S(1)} %get-tuple-element.15, f32[64,1024]{1,0:T(8,128)S(1)} %get-tuple-element.27, f32[192,1024]{1,0:T(8,128)S(1)} %fusion.14, bf16[4,2048,1024]{2,1,0:T(8,128)(2,1)} %param.7, ...), kind=kOutput, calls=%fused_computation.142 | convolution fusion | flops 538771456 | bytes 10228230 | tf_op jit(solution)/shard_map/dot_general | solution.py:21
  118.5 1.3 collective-permute-start.7
  119.8 1.1 collective-permute-done.7
  121.1 5.2 %fusion.180 = f32[64,1024]{1,0:T(8,128)S(1)} fusion(f32[64,1024]{1,0:T(8,128)S(1)} %fusion.183, f32[64,1024]{1,0:T(8,128)S(1)} %get-tuple-element.15, bf16[4,2048,1024]{2,1,0:T(8,128)(2,1)} %param.7, bf16[4,1024,2048]{2,1,0:T(8,128)(2,1)} %param.6, f32[64]{0:T(128)S(1)} %add_rsqrt_fusion.9, f32[1024]{0:T(1024)S(1)} %bitcast.348, pred[]{:T(512)S(6)} %eq.46, ...), kind=kOutput, calls=%fused_computation.141 | convolution fusion | flops 538640384 | bytes 10229760 | tf_op jit(solution)/shard_map/dot_general | solution.py:21
  126.3 2.3 collective-permute-start.8
  128.6 1.1 collective-permute-done.8
  129.9 5.2 %fusion.177 = f32[64,1024]{1,0:T(8,128)S(1)} fusion(f32[64,1024]{1,0:T(8,128)S(1)} %fusion.180, f32[64,1024]{1,0:T(8,128)S(1)} %get-tuple-element.15, bf16[4,2048,1024]{2,1,0:T(8,128)(2,1)} %param.7, bf16[4,1024,2048]{2,1,0:T(8,128)(2,1)} %param.6, f32[64]{0:T(128)S(1)} %add_rsqrt_fusion.8, f32[1024]{0:T(1024)S(1)} %bitcast.349, pred[]{:T(512)S(6)} %eq.23, ...), kind=kOutput, calls=%fused_computation.140 | convolution fusion | flops 538640384 | bytes 10229760 | tf_op jit(solution)/shard_map/dot_general | solution.py:21
  135.1 15.7 %collective-permute-start.16 = (f32[64,1024]{1,0:T(8,128)S(1)}, f32[64,1024]{1,0:T(8,128)S(1)}, u32[]{:S(2)}, u32[]{:S(2)}) collective-permute-start(f32[64,1024]{1,0:T(8,128)S(1)} %fusion.177), channel_id=1, source_target_pairs={{0,16},{4,20},{8,24},{12,28},{1,17},{5,21},{9,25},{13,29},{2,18},{... | collective-permute-start | bytes 786440 | tf_op jit(solution)/shard_map/ppermute | solution.py:12
  150.9 1.3 collective-permute-start.9
  152.2 1.3 compare_select_fusion
  153.5 39.5 %all-reduce = (f32[7]{0:T(128)S(1)}, f32[7]{0:T(128)S(1)}) all-reduce(f32[7]{0:T(128)S(1)} %get-tuple-element.43, f32[7]{0:T(128)S(1)} %get-tuple-element.42), channel_id=1, replica_groups=mesh['layer'=8,'dp'=4] {'layer','dp'}, use_global_device_ids=true, to_apply=%region_18.19 | all-reduce | flops 14 | bytes 112 | tf_op jit(solution)/shard_map/psum | solution.py:259
  193.1 0.1 multiply_reduce_fusion.9
  193.2 5.2 %fusion.201 = f32[64,1024]{1,0:T(8,128)S(1)} fusion(f32[64,1024]{1,0:T(8,128)S(1)} %get-tuple-element.9, bf16[4,2048,1024]{2,1,0:T(8,128)(2,1)} %param.7, bf16[4,1024,2048]{2,1,0:T(8,128)(2,1)} %param.6, f32[64]{0:T(128)S(1)} %add_rsqrt_fusion.7, f32[1024]{0:T(1024)S(1)} %bitcast.353), kind=kOutput, calls=%fused_computation.148 | convolution fusion | flops 538312704 | bytes 9179648 | tf_op jit(solution)/shard_map/dot_general | solution.py:21
  198.4 1.3 collective-permute-start.10
  199.7 0.5 fusion.724
  200.3 4.8 %collective-permute-start.11 = (f32[64,1024]{1,0:T(8,128)S(1)}, f32[64,1024]{1,0:T(8,128)S(1)}, u32[]{:S(2)}, u32[]{:S(2)}) collective-permute-start(f32[64,1024]{1,0:T(8,128)S(1)} %fusion.201), channel_id=1, source_target_pairs={{0,16},{4,20},{8,24},{12,28},{1,17},{5,21},{9,25},{13,29},{2,18},{... | collective-permute-start | bytes 786440 | tf_op jit(solution)/shard_map/ppermute | solution.py:12
  205.2 7.2 %collective-permute-done.11 = f32[64,1024]{1,0:T(8,128)S(1)} collective-permute-done((f32[64,1024]{1,0:T(8,128)S(1)}, f32[64,1024]{1,0:T(8,128)S(1)}, u32[]{:S(2)}, u32[]{:S(2)}) %collective-permute-start.11) | collective-permute-done | bytes 262176 | tf_op jit(solution)/shard_map/ppermute | solution.py:12
  212.6 5.1 %fusion.68 = f32[128,1024]{1,0:T(8,128)S(1)} fusion(bf16[4,2048,1024]{2,1,0:T(8,128)(2,1)} %param.7, bf16[4,1024,2048]{2,1,0:T(8,128)(2,1)} %param.6, f32[128,1024]{1,0:T(8,128)S(1)} %constant_dynamic-update-slice_fusion, f32[1024]{0:T(1024)S(1)} %bitcast.354, f32[128]{0:T(128)S(1)} %add_rsqrt_fusion.4), kind=kOutput, calls=%fused_computation.68 | convolution fusion | flops 1076494336 | bytes 9441792 | tf_op jit(solution)/shard_map/dot_general | solution.py:21
  217.6 0.2 fusion.535
  217.8 5.2 %fusion.210 = f32[64,1024]{1,0:T(8,128)S(1)} fusion(f32[64,1024]{1,0:T(8,128)S(1)} %fusion.201, bf16[4,2048,1024]{2,1,0:T(8,128)(2,1)} %param.7, bf16[4,1024,2048]{2,1,0:T(8,128)(2,1)} %param.6, f32[64]{0:T(128)S(1)} %add_rsqrt_fusion.6, f32[1024]{0:T(1024)S(1)} %bitcast.340), kind=kOutput, calls=%fused_computation.151 | convolution fusion | flops 538312704 | bytes 9179648 | tf_op jit(solution)/shard_map/dot_general | solution.py:21
  223.0 2.0 collective-permute-start.12
  225.0 4.7 %collective-permute-start.13 = (f32[64,1024]{1,0:T(8,128)S(1)}, f32[64,1024]{1,0:T(8,128)S(1)}, u32[]{:S(2)}, u32[]{:S(2)}) collective-permute-start(f32[64,1024]{1,0:T(8,128)S(1)} %fusion.210), channel_id=1, source_target_pairs={{0,16},{4,20},{8,24},{12,28},{1,17},{5,21},{9,25},{13,29},{2,18},{... | collective-permute-start | bytes 786440 | tf_op jit(solution)/shard_map/ppermute | solution.py:12
  229.7 5.8 %fusion = f32[128,1024]{1,0:T(8,128)} fusion(f32[64,1024]{1,0:T(8,128)S(1)} %get-tuple-element.26, f32[64,1024]{1,0:T(8,128)S(1)} %get-tuple-element.9, f32[1024]{0:T(1024)S(1)} %bitcast.350, f32[128]{0:T(128)S(1)} %add_rsqrt_fusion.1, bf16[4,2048,1024]{2,1,0:T(8,128)(2,1)} %param.7, bf16[4,1024,2048]{2,1,0:T(8,128)(2,1)} %param.6), kind=kOutput, calls=%fused_computation | convolution fusion | flops 1076625408 | bytes 9441792 | tf_op jit(solution)/shard_map/dot_general | solution.py:21
  235.5 1.7 collective-permute-done.13
  237.4 5.0 %fusion.52 = f32[128,1024]{1,0:T(8,128)S(1)} fusion(bf16[4,2048,1024]{2,1,0:T(8,128)(2,1)} %param.7, bf16[4,1024,2048]{2,1,0:T(8,128)(2,1)} %param.6, f32[128,1024]{1,0:T(8,128)S(1)} %constant_dynamic-update-slice_fusion.2, f32[1024]{0:T(1024)S(1)} %bitcast.341, f32[128]{0:T(128)S(1)} %add_rsqrt_fusion.3), kind=kOutput, calls=%fused_computation.52 | convolution fusion | flops 1076494336 | bytes 9441792 | tf_op jit(solution)/shard_map/dot_general | solution.py:21
  242.4 0.2 fusion.532
  242.6 5.2 %fusion.219 = f32[64,1024]{1,0:T(8,128)S(1)} fusion(f32[64,1024]{1,0:T(8,128)S(1)} %fusion.210, bf16[4,2048,1024]{2,1,0:T(8,128)(2,1)} %param.7, bf16[4,1024,2048]{2,1,0:T(8,128)(2,1)} %param.6, f32[64]{0:T(128)S(1)} %add_rsqrt_fusion.5, f32[1024]{0:T(1024)S(1)} %bitcast.336), kind=kOutput, calls=%fused_computation.154 | convolution fusion | flops 538312704 | bytes 9179648 | tf_op jit(solution)/shard_map/dot_general | solution.py:21
  247.8 4.4 %collective-permute-start.15 = (f32[64,1024]{1,0:T(8,128)S(1)}, f32[64,1024]{1,0:T(8,128)S(1)}, u32[]{:S(2)}, u32[]{:S(2)}) collective-permute-start(f32[64,1024]{1,0:T(8,128)S(1)} %fusion.219), channel_id=1, source_target_pairs={{0,16},{4,20},{8,24},{12,28},{1,17},{5,21},{9,25},{13,29},{2,18},{... | collective-permute-start | bytes 786440 | tf_op jit(solution)/shard_map/ppermute | solution.py:12
  252.3 1.7 collective-permute-start.14
  253.9 1.1 fusion.526
  255.0 2.0 pad_maximum_fusion
  257.1 3.7 %collective-permute-done.15 = f32[64,1024]{1,0:T(8,128)S(1)} collective-permute-done((f32[64,1024]{1,0:T(8,128)S(1)}, f32[64,1024]{1,0:T(8,128)S(1)}, u32[]{:S(2)}, u32[]{:S(2)}) %collective-permute-start.15) | collective-permute-done | bytes 262176 | tf_op jit(solution)/shard_map/ppermute | solution.py:12
  260.9 5.9 %fusion.36 = f32[128,1024]{1,0:T(8,128)} fusion(bf16[4,2048,1024]{2,1,0:T(8,128)(2,1)} %param.7, bf16[4,1024,2048]{2,1,0:T(8,128)(2,1)} %param.6, f32[128,1024]{1,0:T(8,128)S(1)} %constant_dynamic-update-slice_fusion.4, f32[1024]{0:T(1024)S(1)} %bitcast.337, f32[128]{0:T(128)S(1)} %add_rsqrt_fusion.2), kind=kOutput, calls=%fused_computation.36 | convolution fusion | flops 1076494336 | bytes 9441792 | tf_op jit(solution)/shard_map/dot_general | solution.py:21
  266.8 1.1 fusion.529
  267.9 1.6 maximum_select_fusion
  (49 shorter events, 1.4 us)
Async XLA Ops:
  8.0 29.2 %copy-start = (f32[64,1024]{1,0:T(8,128)S(1)}, f32[64,1024]{1,0:T(8,128)}, u32[]{:S(2)}) copy-start(f32[64,1024]{1,0:T(8,128)} %param.4) | copy-start | bytes 786436
  24.0 13.3 %collective-permute-start.1 = (f32[64,1024]{1,0:T(8,128)S(1)}, f32[64,1024]{1,0:T(8,128)S(1)}, u32[]{:S(2)}, u32[]{:S(2)}) collective-permute-start(f32[64,1024]{1,0:T(8,128)S(1)} %fusion.120), channel_id=1, source_target_pairs={{0,16},{4,20},{8,24},{12,28},{1,17},{5,21},{9,25},{13,29},{2,18},{... | collective-permute-start | bytes 786440 | tf_op jit(solution)/shard_map/ppermute | solution.py:12
  28.9 8.3 %collective-permute-start = (f32[64,1024]{1,0:T(8,128)S(1)}, f32[64,1024]{1,0:T(8,128)S(1)}, u32[]{:S(2)}, u32[]{:S(2)}) collective-permute-start(f32[64,1024]{1,0:T(8,128)S(1)} %fusion.120), channel_id=1, source_target_pairs={{0,4},{4,8},{8,12},{12,16},{16,20},{20,24},{24,28},{1,5},{5,9},{9,... | collective-permute-start | bytes 786440 | tf_op jit(solution)/shard_map/ppermute | solution.py:12
  59.9 2.4 collective-permute-start.2
  67.7 6.8 %collective-permute-start.3 = (f32[64,1024]{1,0:T(8,128)S(1)}, f32[64,1024]{1,0:T(8,128)S(1)}, u32[]{:S(2)}, u32[]{:S(2)}) collective-permute-start(f32[64,1024]{1,0:T(8,128)S(1)} %fusion.192), channel_id=1, source_target_pairs={{0,4},{4,8},{8,12},{12,16},{16,20},{20,24},{24,28},{1,5},{5,9},{9,... | collective-permute-start | bytes 786440 | tf_op jit(solution)/shard_map/ppermute | solution.py:12
  79.8 7.7 %collective-permute-start.4 = (f32[64,1024]{1,0:T(8,128)S(1)}, f32[64,1024]{1,0:T(8,128)S(1)}, u32[]{:S(2)}, u32[]{:S(2)}) collective-permute-start(f32[64,1024]{1,0:T(8,128)S(1)} %fusion.189), channel_id=1, source_target_pairs={{0,4},{4,8},{8,12},{12,16},{16,20},{20,24},{24,28},{1,5},{5,9},{9,... | collective-permute-start | bytes 786440 | tf_op jit(solution)/shard_map/ppermute | solution.py:12
  92.9 15.4 %collective-permute-start.6 = (f32[64,1024]{1,0:T(8,128)S(1)}, f32[64,1024]{1,0:T(8,128)S(1)}, u32[]{:S(2)}, u32[]{:S(2)}) collective-permute-start(f32[64,1024]{1,0:T(8,128)S(1)} %fusion.186), channel_id=1, source_target_pairs={{0,4},{4,8},{8,12},{12,16},{16,20},{20,24},{24,28},{1,5},{5,9},{9,... | collective-permute-start | bytes 786440 | tf_op jit(solution)/shard_map/ppermute | solution.py:12
  99.4 13.7 %collective-permute-start.5 = (f32[64,1024]{1,0:T(8,128)S(1)}, f32[64,1024]{1,0:T(8,128)S(1)}, u32[]{:S(2)}, u32[]{:S(2)}) collective-permute-start(f32[64,1024]{1,0:T(8,128)S(1)} %fusion.186), channel_id=1, source_target_pairs={{0,16},{4,20},{8,24},{12,28},{1,17},{5,21},{9,25},{13,29},{2,18},{... | collective-permute-start | bytes 786440 | tf_op jit(solution)/shard_map/ppermute | solution.py:12
  118.5 2.4 collective-permute-start.7
  126.3 3.4 %collective-permute-start.8 = (f32[64,1024]{1,0:T(8,128)S(1)}, f32[64,1024]{1,0:T(8,128)S(1)}, u32[]{:S(2)}, u32[]{:S(2)}) collective-permute-start(f32[64,1024]{1,0:T(8,128)S(1)} %fusion.180), channel_id=1, source_target_pairs={{0,4},{4,8},{8,12},{12,16},{16,20},{20,24},{24,28},{1,5},{5,9},{9,... | collective-permute-start | bytes 786440 | tf_op jit(solution)/shard_map/ppermute | solution.py:12
  135.1 57.9 %collective-permute-start.16 = (f32[64,1024]{1,0:T(8,128)S(1)}, f32[64,1024]{1,0:T(8,128)S(1)}, u32[]{:S(2)}, u32[]{:S(2)}) collective-permute-start(f32[64,1024]{1,0:T(8,128)S(1)} %fusion.177), channel_id=1, source_target_pairs={{0,16},{4,20},{8,24},{12,28},{1,17},{5,21},{9,25},{13,29},{2,18},{... | collective-permute-start | bytes 786440 | tf_op jit(solution)/shard_map/ppermute | solution.py:12
  150.9 42.2 %collective-permute-start.9 = (f32[64,1024]{1,0:T(8,128)S(1)}, f32[64,1024]{1,0:T(8,128)S(1)}, u32[]{:S(2)}, u32[]{:S(2)}) collective-permute-start(f32[64,1024]{1,0:T(8,128)S(1)} %fusion.177), channel_id=1, source_target_pairs={{0,4},{4,8},{8,12},{12,16},{16,20},{20,24},{24,28},{1,5},{5,9},{9,... | collective-permute-start | bytes 786440 | tf_op jit(solution)/shard_map/ppermute | solution.py:12
  198.4 6.8 %collective-permute-start.10 = (f32[64,1024]{1,0:T(8,128)S(1)}, f32[64,1024]{1,0:T(8,128)S(1)}, u32[]{:S(2)}, u32[]{:S(2)}) collective-permute-start(f32[64,1024]{1,0:T(8,128)S(1)} %fusion.201), channel_id=1, source_target_pairs={{0,4},{4,8},{8,12},{12,16},{16,20},{20,24},{24,28},{1,5},{5,9},{9,... | collective-permute-start | bytes 786440 | tf_op jit(solution)/shard_map/ppermute | solution.py:12
  200.3 12.2 %collective-permute-start.11 = (f32[64,1024]{1,0:T(8,128)S(1)}, f32[64,1024]{1,0:T(8,128)S(1)}, u32[]{:S(2)}, u32[]{:S(2)}) collective-permute-start(f32[64,1024]{1,0:T(8,128)S(1)} %fusion.201), channel_id=1, source_target_pairs={{0,16},{4,20},{8,24},{12,28},{1,17},{5,21},{9,25},{13,29},{2,18},{... | collective-permute-start | bytes 786440 | tf_op jit(solution)/shard_map/ppermute | solution.py:12
  223.0 19.6 %copy-start.1 = (f32[64,1024]{1,0:T(8,128)}, f32[64,1024]{1,0:T(8,128)S(1)}, u32[]{:S(2)}) copy-start(f32[64,1024]{1,0:T(8,128)S(1)} %fusion.210) | copy-start | bytes 786436
  223.0 12.5 %collective-permute-start.12 = (f32[64,1024]{1,0:T(8,128)S(1)}, f32[64,1024]{1,0:T(8,128)S(1)}, u32[]{:S(2)}, u32[]{:S(2)}) collective-permute-start(f32[64,1024]{1,0:T(8,128)S(1)} %fusion.210), channel_id=1, source_target_pairs={{0,4},{4,8},{8,12},{12,16},{16,20},{20,24},{24,28},{1,5},{5,9},{9,... | collective-permute-start | bytes 786440 | tf_op jit(solution)/shard_map/ppermute | solution.py:12
  225.0 12.2 %collective-permute-start.13 = (f32[64,1024]{1,0:T(8,128)S(1)}, f32[64,1024]{1,0:T(8,128)S(1)}, u32[]{:S(2)}, u32[]{:S(2)}) collective-permute-start(f32[64,1024]{1,0:T(8,128)S(1)} %fusion.210), channel_id=1, source_target_pairs={{0,16},{4,20},{8,24},{12,28},{1,17},{5,21},{9,25},{13,29},{2,18},{... | collective-permute-start | bytes 786440 | tf_op jit(solution)/shard_map/ppermute | solution.py:12
  247.8 12.9 %collective-permute-start.15 = (f32[64,1024]{1,0:T(8,128)S(1)}, f32[64,1024]{1,0:T(8,128)S(1)}, u32[]{:S(2)}, u32[]{:S(2)}) collective-permute-start(f32[64,1024]{1,0:T(8,128)S(1)} %fusion.219), channel_id=1, source_target_pairs={{0,16},{4,20},{8,24},{12,28},{1,17},{5,21},{9,25},{13,29},{2,18},{... | collective-permute-start | bytes 786440 | tf_op jit(solution)/shard_map/ppermute | solution.py:12
  252.3 4.8 %collective-permute-start.14 = (f32[64,1024]{1,0:T(8,128)S(1)}, f32[64,1024]{1,0:T(8,128)S(1)}, u32[]{:S(2)}, u32[]{:S(2)}) collective-permute-start(f32[64,1024]{1,0:T(8,128)S(1)} %fusion.219), channel_id=1, source_target_pairs={{0,4},{4,8},{8,12},{12,16},{16,20},{20,24},{24,28},{1,5},{5,9},{9,... | collective-permute-start | bytes 786440 | tf_op jit(solution)/shard_map/ppermute | solution.py:12
where the time goes:
time: 270 us; the launch traced here: 269 us
  matrix products  112 us (41%)
  starting transfers between devices  74.9 us (28%)
  blocking collectives  39.5 us (15%)
  waiting for transfers between devices  29.7 us (11%)
  other arithmetic  11.6 us (4%)
    dot_general x21, matrix products, branch(): return jnp.dot(hidden, weight_out, preferred_element_type=jnp.float32)  112 us
    ppermute x17, starting transfers between devices, shifted(): return lax.ppermute(block, axis, route)  74.9 us
    psum x1, blocking collectives, local_quads(): lax.psum((gap_sum * one_hot, step_sum * one_hot), ('layer', 'dp'))  39.5 us
    ppermute x17, waiting for transfers between devices, shifted(): return lax.ppermute(block, axis, route)  29.7 us
  transfers between devices with their start and end apart: 17, of which 10 were waited for; matrix products, arithmetic and copies ran while one was open for 4% of the time, Pallas kernels for 0%

commit v1 on v0

--- a/solution.py
+++ b/solution.py
@@ -4,6 +4,7 @@
 from jax.sharding import PartitionSpec as P
 
 epsilon = 1e-06
+measure_axis_part_for = lambda z: lax.psum(lax.psum(z, "dp"), "layer")
 
 
 def shifted(block, axis, distance):
@@ -256,7 +257,7 @@
     defects_four = jnp.where((points >= 4)[:, None, None], jnp.stack(fours), 0.0)
     defects_sixteen = jnp.where((points >= 16)[:, None, None], jnp.stack(sixteens), 0.0)
     one_hot = (jnp.arange(sections - 1) == here - 1).astype(jnp.float32)
-    gap_total, step_total = lax.psum((gap_sum * one_hot, step_sum * one_hot), ("layer", "dp"))
+    gap_total, step_total = measure_axis_part_for((gap_sum * one_hot, step_sum * one_hot))
     ratios = jnp.sqrt(gap_total / (step_total + epsilon))
     return (jnp.stack(states), ratios, defects_four, defects_sixteen)
 

time: 270 us -> 253 us (0.937)
  blocking collectives: 39.5 us -> 23.7 us
    psum x1 -> x2, blocking collectives: 39.5 us -> 23.7 us  [measure_axis_part_for = lambda z: lax.psum(lax.psum(z, 'dp'), 'layer')]
where the time goes in v1:
time: 253 us; the launch traced here: 252 us
  matrix products  112 us (44%)
  starting transfers between devices  73.1 us (29%)
  waiting for transfers between devices  29.8 us (12%)
  blocking collectives  23.7 us (9%)
  other arithmetic  11.6 us (5%)
    dot_general x21, matrix products, branch(): return jnp.dot(hidden, weight_out, preferred_element_type=jnp.float32)  112 us
    ppermute x17, starting transfers between devices, shifted(): return lax.ppermute(block, axis, route)  73.1 us
    ppermute x17, waiting for transfers between devices, shifted(): return lax.ppermute(block, axis, route)  29.8 us
    psum x2, blocking collectives, measure_axis_part_for = lambda z: lax.psum(lax.psum(z, 'dp'), 'layer')  23.7 us
  transfers between devices with their start and end apart: 17, of which 10 were waited for; matrix products, arithmetic and copies ran while one was open for 4% of the time, Pallas kernels for 0%

profile of v1, /device:TPU:0, one launch (start us, length us, event | category | flops | bytes accessed | tf_op | source)
XLA Modules:
  0.0 252.0 jit_solution(6070104555537408343)
XLA Ops:
  0.6 1.1 multiply_reduce_fusion.22
  1.7 0.9 fusion.815
  2.6 5.4 %multiply_reduce_fusion.21 = (f32[64]{0:T(128)S(1)}, f32[64,1024]{1,0:T(8,128)S(1)}) fusion(f32[64,1024]{1,0:T(8,128)} %param.4, bf16[4,2048,1024]{2,1,0:T(8,128)(2,1)} %param.7, bf16[4,1024,2048]{2,1,0:T(8,128)(2,1)} %param.6, f32[1024]{0:T(1024)S(1)} %bitcast.351, f32[64]{0:T(128)S(1)} %add_rsqrt_fusion.20), kind=kOutput, calls=%fused_computation.443 | convolution fusion | flops 538443712 | bytes 9179648 | tf_op jit(solution)/shard_map/dot_general | solution.py:22
  8.0 5.4 %multiply_reduce_fusion.20 = (f32[64]{0:T(128)S(1)}, f32[64,1024]{1,0:T(8,128)S(1)}) fusion(f32[64,1024]{1,0:T(8,128)S(1)} %get-tuple-element.35, bf16[4,2048,1024]{2,1,0:T(8,128)(2,1)} %param.7, bf16[4,1024,2048]{2,1,0:T(8,128)(2,1)} %param.6, f32[1024]{0:T(1024)S(1)} %bitcast.338, f32[64]{0:T(128)S(1)} %add_rsqrt_fusion.19), kind=kOutput, calls=%fused_computation.441 | convolution fusion | flops 538443712 | bytes 9179904 | tf_op jit(solution)/shard_map/dot_general | solution.py:22
  13.4 5.3 %multiply_reduce_fusion.19 = (f32[64]{0:T(128)S(1)}, f32[64,1024]{1,0:T(8,128)S(1)}) fusion(f32[64,1024]{1,0:T(8,128)S(1)} %get-tuple-element.37, bf16[4,2048,1024]{2,1,0:T(8,128)(2,1)} %param.7, bf16[4,1024,2048]{2,1,0:T(8,128)(2,1)} %param.6, f32[1024]{0:T(1024)S(1)} %bitcast.334, f32[64]{0:T(128)S(1)} %add_rsqrt_fusion.18), kind=kOutput, calls=%fused_computation.439 | convolution fusion | flops 538443712 | bytes 9179904 | tf_op jit(solution)/shard_map/dot_general | solution.py:22
  18.8 5.2 %fusion.120 = f32[64,1024]{1,0:T(8,128)S(1)} fusion(f32[64,1024]{1,0:T(8,128)S(1)} %get-tuple-element.39, bf16[4,2048,1024]{2,1,0:T(8,128)(2,1)} %param.7, bf16[4,1024,2048]{2,1,0:T(8,128)(2,1)} %param.6, f32[1024]{0:T(1024)S(1)} %bitcast.342, f32[64]{0:T(128)S(1)} %add_rsqrt_fusion.17), kind=kOutput, calls=%fused_computation.121 | convolution fusion | flops 538312704 | bytes 9179648 | tf_op jit(solution)/shard_map/dot_general | solution.py:22
  24.0 4.9 %collective-permute-start.1 = (f32[64,1024]{1,0:T(8,128)S(1)}, f32[64,1024]{1,0:T(8,128)S(1)}, u32[]{:S(2)}, u32[]{:S(2)}) collective-permute-start(f32[64,1024]{1,0:T(8,128)S(1)} %fusion.120), channel_id=1, source_target_pairs={{0,16},{4,20},{8,24},{12,28},{1,17},{5,21},{9,25},{13,29},{2,18},{... | collective-permute-start | bytes 786440 | tf_op jit(solution)/shard_map/ppermute | solution.py:13
  28.9 1.7 collective-permute-start
  30.6 6.7 %collective-permute-done.1 = f32[64,1024]{1,0:T(8,128)S(1)} collective-permute-done((f32[64,1024]{1,0:T(8,128)S(1)}, f32[64,1024]{1,0:T(8,128)S(1)}, u32[]{:S(2)}, u32[]{:S(2)}) %collective-permute-start.1) | collective-permute-done | bytes 262176 | tf_op jit(solution)/shard_map/ppermute | solution.py:13
  37.2 0.1 multiply_reduce_fusion.18
  37.4 5.3 %multiply_reduce_fusion.17 = (f32[64]{0:T(128)S(1)}, f32[64,1024]{1,0:T(8,128)S(1)}) fusion(f32[64,1024]{1,0:T(8,128)S(1)} %get-tuple-element.15, bf16[4,2048,1024]{2,1,0:T(8,128)(2,1)} %param.7, bf16[4,1024,2048]{2,1,0:T(8,128)(2,1)} %param.6, f32[64]{0:T(128)S(1)} %add_rsqrt_fusion.16, f32[1024]{0:T(1024)S(1)} %bitcast.352), kind=kOutput, calls=%fused_computation.435 | convolution fusion | flops 538443712 | bytes 9179904 | tf_op jit(solution)/shard_map/dot_general | solution.py:22
  42.7 5.3 %multiply_reduce_fusion.16 = (f32[64]{0:T(128)S(1)}, f32[64,1024]{1,0:T(8,128)S(1)}) fusion(f32[64,1024]{1,0:T(8,128)S(1)} %get-tuple-element.41, bf16[4,2048,1024]{2,1,0:T(8,128)(2,1)} %param.7, bf16[4,1024,2048]{2,1,0:T(8,128)(2,1)} %param.6, f32[64]{0:T(128)S(1)} %add_rsqrt_fusion.15, f32[1024]{0:T(1024)S(1)} %bitcast.339), kind=kOutput, calls=%fused_computation.433 | convolution fusion | flops 538443712 | bytes 9179904 | tf_op jit(solution)/shard_map/dot_general | solution.py:22
  48.1 5.2 %fusion.216 = f32[64,1024]{1,0:T(8,128)S(1)} fusion(f32[64,1024]{1,0:T(8,128)S(1)} %get-tuple-element.43, bf16[4,2048,1024]{2,1,0:T(8,128)(2,1)} %param.7, bf16[4,1024,2048]{2,1,0:T(8,128)(2,1)} %param.6, f32[64]{0:T(128)S(1)} %add_rsqrt_fusion.14, f32[1024]{0:T(1024)S(1)} %bitcast.335), kind=kOutput, calls=%fused_computation.153 | convolution fusion | flops 538312704 | bytes 9179648 | tf_op jit(solution)/shard_map/dot_general | solution.py:22
  53.5 5.7 %fusion.14 = f32[192,1024]{1,0:T(8,128)S(1)} fusion(f32[64,1024]{1,0:T(8,128)S(1)} %get-tuple-element.29, f32[64,1024]{1,0:T(8,128)S(1)} %get-tuple-element.15, f32[64,1024]{1,0:T(8,128)S(1)} %fusion.216, f32[1024]{0:T(1024)S(1)} %bitcast.343, f32[192]{0:T(256)S(1)} %add_rsqrt_fusion, bf16[4,2048,1024]{2,1,0:T(8,128)(2,1)} %param.7, ...), kind=kOutput, calls=%fused_computation.14 | convolution fusion | flops 1615134720 | bytes 9966336 | tf_op jit(solution)/shard_map/dot_general | solution.py:22
  59.2 0.7 multiply_reduce_fusion.5
  59.9 1.3 collective-permute-start.2
  61.2 1.1 collective-permute-done.2
  62.4 5.2 %fusion.192 = f32[64,1024]{1,0:T(8,128)S(1)} fusion(f32[64,1024]{1,0:T(8,128)S(1)} %get-tuple-element.16, f32[64,1024]{1,0:T(8,128)S(1)} %get-tuple-element.17, bf16[4,2048,1024]{2,1,0:T(8,128)(2,1)} %param.7, bf16[4,1024,2048]{2,1,0:T(8,128)(2,1)} %param.6, f32[64]{0:T(128)S(1)} %add_rsqrt_fusion.13, f32[1024]{0:T(1024)S(1)} %bitcast.344, pred[]{:T(512)S(6)} %eq.46, ...), kind=kOutput, calls=%fused_computation.145 | convolution fusion | flops 538640384 | bytes 10229760 | tf_op jit(solution)/shard_map/dot_general | solution.py:22
  67.7 5.6 %collective-permute-start.3 = (f32[64,1024]{1,0:T(8,128)S(1)}, f32[64,1024]{1,0:T(8,128)S(1)}, u32[]{:S(2)}, u32[]{:S(2)}) collective-permute-start(f32[64,1024]{1,0:T(8,128)S(1)} %fusion.192), channel_id=1, source_target_pairs={{0,4},{4,8},{8,12},{12,16},{16,20},{20,24},{24,28},{1,5},{5,9},{9,... | collective-permute-start | bytes 786440 | tf_op jit(solution)/shard_map/ppermute | solution.py:13
  73.3 1.1 collective-permute-done.3
  74.6 5.2 %fusion.189 = f32[64,1024]{1,0:T(8,128)S(1)} fusion(f32[64,1024]{1,0:T(8,128)S(1)} %fusion.192, f32[64,1024]{1,0:T(8,128)S(1)} %get-tuple-element.17, bf16[4,2048,1024]{2,1,0:T(8,128)(2,1)} %param.7, bf16[4,1024,2048]{2,1,0:T(8,128)(2,1)} %param.6, f32[64]{0:T(128)S(1)} %add_rsqrt_fusion.12, f32[1024]{0:T(1024)S(1)} %bitcast.345, pred[]{:T(512)S(6)} %eq.23, ...), kind=kOutput, calls=%fused_computation.144 | convolution fusion | flops 538640384 | bytes 10229760 | tf_op jit(solution)/shard_map/dot_general | solution.py:22
  79.8 6.6 %collective-permute-start.4 = (f32[64,1024]{1,0:T(8,128)S(1)}, f32[64,1024]{1,0:T(8,128)S(1)}, u32[]{:S(2)}, u32[]{:S(2)}) collective-permute-start(f32[64,1024]{1,0:T(8,128)S(1)} %fusion.189), channel_id=1, source_target_pairs={{0,4},{4,8},{8,12},{12,16},{16,20},{20,24},{24,28},{1,5},{5,9},{9,... | collective-permute-start | bytes 786440 | tf_op jit(solution)/shard_map/ppermute | solution.py:13
  86.4 1.1 collective-permute-done.4
  87.6 5.2 %fusion.186 = f32[64,1024]{1,0:T(8,128)S(1)} fusion(f32[64,1024]{1,0:T(8,128)S(1)} %fusion.189, f32[64,1024]{1,0:T(8,128)S(1)} %get-tuple-element.17, bf16[4,2048,1024]{2,1,0:T(8,128)(2,1)} %param.7, bf16[4,1024,2048]{2,1,0:T(8,128)(2,1)} %param.6, f32[64]{0:T(128)S(1)} %add_rsqrt_fusion.11, f32[1024]{0:T(1024)S(1)} %bitcast.346, pred[]{:T(512)S(6)} %eq.49, ...), kind=kOutput, calls=%fused_computation.143 | convolution fusion | flops 538640384 | bytes 10229760 | tf_op jit(solution)/shard_map/dot_general | solution.py:22
  92.9 6.6 %collective-permute-start.6 = (f32[64,1024]{1,0:T(8,128)S(1)}, f32[64,1024]{1,0:T(8,128)S(1)}, u32[]{:S(2)}, u32[]{:S(2)}) collective-permute-start(f32[64,1024]{1,0:T(8,128)S(1)} %fusion.186), channel_id=1, source_target_pairs={{0,4},{4,8},{8,12},{12,16},{16,20},{20,24},{24,28},{1,5},{5,9},{9,... | collective-permute-start | bytes 786440 | tf_op jit(solution)/shard_map/ppermute | solution.py:13
  99.4 8.8 %collective-permute-start.5 = (f32[64,1024]{1,0:T(8,128)S(1)}, f32[64,1024]{1,0:T(8,128)S(1)}, u32[]{:S(2)}, u32[]{:S(2)}) collective-permute-start(f32[64,1024]{1,0:T(8,128)S(1)} %fusion.186), channel_id=1, source_target_pairs={{0,16},{4,20},{8,24},{12,28},{1,17},{5,21},{9,25},{13,29},{2,18},{... | collective-permute-start | bytes 786440 | tf_op jit(solution)/shard_map/ppermute | solution.py:13
  108.3 4.8 %collective-permute-done.5 = f32[64,1024]{1,0:T(8,128)S(1)} collective-permute-done((f32[64,1024]{1,0:T(8,128)S(1)}, f32[64,1024]{1,0:T(8,128)S(1)}, u32[]{:S(2)}, u32[]{:S(2)}) %collective-permute-start.5) | collective-permute-done | bytes 262176 | tf_op jit(solution)/shard_map/ppermute | solution.py:13
  113.1 0.1 multiply_reduce_fusion.12
  113.3 5.3 %fusion.183 = f32[64,1024]{1,0:T(8,128)S(1)} fusion(f32[64,1024]{1,0:T(8,128)S(1)} %fusion.186, f32[64,1024]{1,0:T(8,128)S(1)} %get-tuple-element.13, f32[64,1024]{1,0:T(8,128)S(1)} %get-tuple-element.17, f32[64,1024]{1,0:T(8,128)S(1)} %get-tuple-element.29, f32[192,1024]{1,0:T(8,128)S(1)} %fusion.14, bf16[4,2048,1024]{2,1,0:T(8,128)(2,1)} %param.7, ...), kind=kOutput, calls=%fused_computation.142 | convolution fusion | flops 538771456 | bytes 10228230 | tf_op jit(solution)/shard_map/dot_general | solution.py:22
  118.5 1.3 collective-permute-start.7
  119.8 1.1 collective-permute-done.7
  121.1 5.2 %fusion.180 = f32[64,1024]{1,0:T(8,128)S(1)} fusion(f32[64,1024]{1,0:T(8,128)S(1)} %fusion.183, f32[64,1024]{1,0:T(8,128)S(1)} %get-tuple-element.17, bf16[4,2048,1024]{2,1,0:T(8,128)(2,1)} %param.7, bf16[4,1024,2048]{2,1,0:T(8,128)(2,1)} %param.6, f32[64]{0:T(128)S(1)} %add_rsqrt_fusion.9, f32[1024]{0:T(1024)S(1)} %bitcast.348, pred[]{:T(512)S(6)} %eq.46, ...), kind=kOutput, calls=%fused_computation.141 | convolution fusion | flops 538640384 | bytes 10229760 | tf_op jit(solution)/shard_map/dot_general | solution.py:22
  126.3 2.3 collective-permute-start.8
  128.6 1.1 collective-permute-done.8
  129.9 5.2 %fusion.177 = f32[64,1024]{1,0:T(8,128)S(1)} fusion(f32[64,1024]{1,0:T(8,128)S(1)} %fusion.180, f32[64,1024]{1,0:T(8,128)S(1)} %get-tuple-element.17, bf16[4,2048,1024]{2,1,0:T(8,128)(2,1)} %param.7, bf16[4,1024,2048]{2,1,0:T(8,128)(2,1)} %param.6, f32[64]{0:T(128)S(1)} %add_rsqrt_fusion.8, f32[1024]{0:T(1024)S(1)} %bitcast.349, pred[]{:T(512)S(6)} %eq.23, ...), kind=kOutput, calls=%fused_computation.140 | convolution fusion | flops 538640384 | bytes 10229760 | tf_op jit(solution)/shard_map/dot_general | solution.py:22
  135.1 15.7 %collective-permute-start.16 = (f32[64,1024]{1,0:T(8,128)S(1)}, f32[64,1024]{1,0:T(8,128)S(1)}, u32[]{:S(2)}, u32[]{:S(2)}) collective-permute-start(f32[64,1024]{1,0:T(8,128)S(1)} %fusion.177), channel_id=1, source_target_pairs={{0,16},{4,20},{8,24},{12,28},{1,17},{5,21},{9,25},{13,29},{2,18},{... | collective-permute-start | bytes 786440 | tf_op jit(solution)/shard_map/ppermute | solution.py:13
  150.9 1.3 collective-permute-start.9
  152.2 1.3 compare_select_fusion
  153.5 12.0 %all-reduce.1 = (f32[7]{0:T(128)S(1)}, f32[7]{0:T(128)S(1)}) all-reduce(f32[7]{0:T(128)S(1)} %get-tuple-element.45, f32[7]{0:T(128)S(1)} %get-tuple-element.44), channel_id=1, replica_groups=mesh['layer'=8,'dp'=4] {'dp'}, use_global_device_ids=true, to_apply=%region_18.19 | all-reduce | flops 14 | bytes 112 | tf_op jit(solution)/shard_map/psum | solution.py:7
  165.5 11.8 %all-reduce = (f32[7]{0:T(128)S(1)}, f32[7]{0:T(128)S(1)}) all-reduce(f32[7]{0:T(128)S(1)} %get-tuple-element.8, f32[7]{0:T(128)S(1)} %get-tuple-element.9), channel_id=1, replica_groups=mesh['layer'=8,'dp'=4] {'layer'}, use_global_device_ids=true, to_apply=%region_19.20 | all-reduce | flops 14 | bytes 112 | tf_op jit(solution)/shard_map/psum | solution.py:7
  177.3 0.1 multiply_reduce_fusion.9
  177.4 5.2 %fusion.201 = f32[64,1024]{1,0:T(8,128)S(1)} fusion(f32[64,1024]{1,0:T(8,128)S(1)} %get-tuple-element.11, bf16[4,2048,1024]{2,1,0:T(8,128)(2,1)} %param.7, bf16[4,1024,2048]{2,1,0:T(8,128)(2,1)} %param.6, f32[64]{0:T(128)S(1)} %add_rsqrt_fusion.7, f32[1024]{0:T(1024)S(1)} %bitcast.353), kind=kOutput, calls=%fused_computation.148 | convolution fusion | flops 538312704 | bytes 9179648 | tf_op jit(solution)/shard_map/dot_general | solution.py:22
  182.6 1.8 collective-permute-start.10
  184.4 0.5 fusion.724
  185.0 2.6 %collective-permute-start.11 = (f32[64,1024]{1,0:T(8,128)S(1)}, f32[64,1024]{1,0:T(8,128)S(1)}, u32[]{:S(2)}, u32[]{:S(2)}) collective-permute-start(f32[64,1024]{1,0:T(8,128)S(1)} %fusion.201), channel_id=1, source_target_pairs={{0,16},{4,20},{8,24},{12,28},{1,17},{5,21},{9,25},{13,29},{2,18},{... | collective-permute-start | bytes 786440 | tf_op jit(solution)/shard_map/ppermute | solution.py:13
  187.8 7.2 %collective-permute-done.11 = f32[64,1024]{1,0:T(8,128)S(1)} collective-permute-done((f32[64,1024]{1,0:T(8,128)S(1)}, f32[64,1024]{1,0:T(8,128)S(1)}, u32[]{:S(2)}, u32[]{:S(2)}) %collective-permute-start.11) | collective-permute-done | bytes 262176 | tf_op jit(solution)/shard_map/ppermute | solution.py:13
  195.1 5.1 %fusion.68 = f32[128,1024]{1,0:T(8,128)S(1)} fusion(bf16[4,2048,1024]{2,1,0:T(8,128)(2,1)} %param.7, bf16[4,1024,2048]{2,1,0:T(8,128)(2,1)} %param.6, f32[128,1024]{1,0:T(8,128)S(1)} %constant_dynamic-update-slice_fusion, f32[1024]{0:T(1024)S(1)} %bitcast.354, f32[128]{0:T(128)S(1)} %add_rsqrt_fusion.4), kind=kOutput, calls=%fused_computation.68 | convolution fusion | flops 1076494336 | bytes 9441792 | tf_op jit(solution)/shard_map/dot_general | solution.py:22
  200.2 0.2 fusion.535
  200.3 5.2 %fusion.210 = f32[64,1024]{1,0:T(8,128)S(1)} fusion(f32[64,1024]{1,0:T(8,128)S(1)} %fusion.201, bf16[4,2048,1024]{2,1,0:T(8,128)(2,1)} %param.7, bf16[4,1024,2048]{2,1,0:T(8,128)(2,1)} %param.6, f32[64]{0:T(128)S(1)} %add_rsqrt_fusion.6, f32[1024]{0:T(1024)S(1)} %bitcast.340), kind=kOutput, calls=%fused_computation.151 | convolution fusion | flops 538312704 | bytes 9179648 | tf_op jit(solution)/shard_map/dot_general | solution.py:22
  205.6 1.9 collective-permute-start.12
  207.5 4.6 %collective-permute-start.13 = (f32[64,1024]{1,0:T(8,128)S(1)}, f32[64,1024]{1,0:T(8,128)S(1)}, u32[]{:S(2)}, u32[]{:S(2)}) collective-permute-start(f32[64,1024]{1,0:T(8,128)S(1)} %fusion.210), channel_id=1, source_target_pairs={{0,16},{4,20},{8,24},{12,28},{1,17},{5,21},{9,25},{13,29},{2,18},{... | collective-permute-start | bytes 786440 | tf_op jit(solution)/shard_map/ppermute | solution.py:13
  212.2 5.8 %fusion = f32[128,1024]{1,0:T(8,128)} fusion(f32[64,1024]{1,0:T(8,128)S(1)} %get-tuple-element.28, f32[64,1024]{1,0:T(8,128)S(1)} %get-tuple-element.11, f32[1024]{0:T(1024)S(1)} %bitcast.350, f32[128]{0:T(128)S(1)} %add_rsqrt_fusion.1, bf16[4,2048,1024]{2,1,0:T(8,128)(2,1)} %param.7, bf16[4,1024,2048]{2,1,0:T(8,128)(2,1)} %param.6), kind=kOutput, calls=%fused_computation | convolution fusion | flops 1076625408 | bytes 9441792 | tf_op jit(solution)/shard_map/dot_general | solution.py:22
  218.0 1.7 collective-permute-done.13
  219.9 5.0 %fusion.52 = f32[128,1024]{1,0:T(8,128)S(1)} fusion(bf16[4,2048,1024]{2,1,0:T(8,128)(2,1)} %param.7, bf16[4,1024,2048]{2,1,0:T(8,128)(2,1)} %param.6, f32[128,1024]{1,0:T(8,128)S(1)} %constant_dynamic-update-slice_fusion.2, f32[1024]{0:T(1024)S(1)} %bitcast.341, f32[128]{0:T(128)S(1)} %add_rsqrt_fusion.3), kind=kOutput, calls=%fused_computation.52 | convolution fusion | flops 1076494336 | bytes 9441792 | tf_op jit(solution)/shard_map/dot_general | solution.py:22
  225.0 0.2 fusion.532
  225.2 5.2 %fusion.219 = f32[64,1024]{1,0:T(8,128)S(1)} fusion(f32[64,1024]{1,0:T(8,128)S(1)} %fusion.210, bf16[4,2048,1024]{2,1,0:T(8,128)(2,1)} %param.7, bf16[4,1024,2048]{2,1,0:T(8,128)(2,1)} %param.6, f32[64]{0:T(128)S(1)} %add_rsqrt_fusion.5, f32[1024]{0:T(1024)S(1)} %bitcast.336), kind=kOutput, calls=%fused_computation.154 | convolution fusion | flops 538312704 | bytes 9179648 | tf_op jit(solution)/shard_map/dot_general | solution.py:22
  230.4 4.4 %collective-permute-start.15 = (f32[64,1024]{1,0:T(8,128)S(1)}, f32[64,1024]{1,0:T(8,128)S(1)}, u32[]{:S(2)}, u32[]{:S(2)}) collective-permute-start(f32[64,1024]{1,0:T(8,128)S(1)} %fusion.219), channel_id=1, source_target_pairs={{0,16},{4,20},{8,24},{12,28},{1,17},{5,21},{9,25},{13,29},{2,18},{... | collective-permute-start | bytes 786440 | tf_op jit(solution)/shard_map/ppermute | solution.py:13
  234.8 1.7 collective-permute-start.14
  236.5 1.1 fusion.526
  237.6 2.0 pad_maximum_fusion
  239.6 3.7 %collective-permute-done.15 = f32[64,1024]{1,0:T(8,128)S(1)} collective-permute-done((f32[64,1024]{1,0:T(8,128)S(1)}, f32[64,1024]{1,0:T(8,128)S(1)}, u32[]{:S(2)}, u32[]{:S(2)}) %collective-permute-start.15) | collective-permute-done | bytes 262176 | tf_op jit(solution)/shard_map/ppermute | solution.py:13
  243.5 5.9 %fusion.36 = f32[128,1024]{1,0:T(8,128)} fusion(bf16[4,2048,1024]{2,1,0:T(8,128)(2,1)} %param.7, bf16[4,1024,2048]{2,1,0:T(8,128)(2,1)} %param.6, f32[128,1024]{1,0:T(8,128)S(1)} %constant_dynamic-update-slice_fusion.4, f32[1024]{0:T(1024)S(1)} %bitcast.337, f32[128]{0:T(128)S(1)} %add_rsqrt_fusion.2), kind=kOutput, calls=%fused_computation.36 | convolution fusion | flops 1076494336 | bytes 9441792 | tf_op jit(solution)/shard_map/dot_general | solution.py:22
  249.3 1.1 fusion.529
  250.4 1.6 maximum_select_fusion
  (50 shorter events, 1.6 us)
Async XLA Ops:
  8.0 29.2 %copy-start = (f32[64,1024]{1,0:T(8,128)S(1)}, f32[64,1024]{1,0:T(8,128)}, u32[]{:S(2)}) copy-start(f32[64,1024]{1,0:T(8,128)} %param.4) | copy-start | bytes 786436
  24.0 13.3 %collective-permute-start.1 = (f32[64,1024]{1,0:T(8,128)S(1)}, f32[64,1024]{1,0:T(8,128)S(1)}, u32[]{:S(2)}, u32[]{:S(2)}) collective-permute-start(f32[64,1024]{1,0:T(8,128)S(1)} %fusion.120), channel_id=1, source_target_pairs={{0,16},{4,20},{8,24},{12,28},{1,17},{5,21},{9,25},{13,29},{2,18},{... | collective-permute-start | bytes 786440 | tf_op jit(solution)/shard_map/ppermute | solution.py:13
  28.9 8.3 %collective-permute-start = (f32[64,1024]{1,0:T(8,128)S(1)}, f32[64,1024]{1,0:T(8,128)S(1)}, u32[]{:S(2)}, u32[]{:S(2)}) collective-permute-start(f32[64,1024]{1,0:T(8,128)S(1)} %fusion.120), channel_id=1, source_target_pairs={{0,4},{4,8},{8,12},{12,16},{16,20},{20,24},{24,28},{1,5},{5,9},{9,... | collective-permute-start | bytes 786440 | tf_op jit(solution)/shard_map/ppermute | solution.py:13
  59.9 2.4 collective-permute-start.2
  67.7 6.8 %collective-permute-start.3 = (f32[64,1024]{1,0:T(8,128)S(1)}, f32[64,1024]{1,0:T(8,128)S(1)}, u32[]{:S(2)}, u32[]{:S(2)}) collective-permute-start(f32[64,1024]{1,0:T(8,128)S(1)} %fusion.192), channel_id=1, source_target_pairs={{0,4},{4,8},{8,12},{12,16},{16,20},{20,24},{24,28},{1,5},{5,9},{9,... | collective-permute-start | bytes 786440 | tf_op jit(solution)/shard_map/ppermute | solution.py:13
  79.8 7.7 %collective-permute-start.4 = (f32[64,1024]{1,0:T(8,128)S(1)}, f32[64,1024]{1,0:T(8,128)S(1)}, u32[]{:S(2)}, u32[]{:S(2)}) collective-permute-start(f32[64,1024]{1,0:T(8,128)S(1)} %fusion.189), channel_id=1, source_target_pairs={{0,4},{4,8},{8,12},{12,16},{16,20},{20,24},{24,28},{1,5},{5,9},{9,... | collective-permute-start | bytes 786440 | tf_op jit(solution)/shard_map/ppermute | solution.py:13
  92.9 15.4 %collective-permute-start.6 = (f32[64,1024]{1,0:T(8,128)S(1)}, f32[64,1024]{1,0:T(8,128)S(1)}, u32[]{:S(2)}, u32[]{:S(2)}) collective-permute-start(f32[64,1024]{1,0:T(8,128)S(1)} %fusion.186), channel_id=1, source_target_pairs={{0,4},{4,8},{8,12},{12,16},{16,20},{20,24},{24,28},{1,5},{5,9},{9,... | collective-permute-start | bytes 786440 | tf_op jit(solution)/shard_map/ppermute | solution.py:13
  99.4 13.7 %collective-permute-start.5 = (f32[64,1024]{1,0:T(8,128)S(1)}, f32[64,1024]{1,0:T(8,128)S(1)}, u32[]{:S(2)}, u32[]{:S(2)}) collective-permute-start(f32[64,1024]{1,0:T(8,128)S(1)} %fusion.186), channel_id=1, source_target_pairs={{0,16},{4,20},{8,24},{12,28},{1,17},{5,21},{9,25},{13,29},{2,18},{... | collective-permute-start | bytes 786440 | tf_op jit(solution)/shard_map/ppermute | solution.py:13
  118.5 2.4 collective-permute-start.7
  126.3 3.4 %collective-permute-start.8 = (f32[64,1024]{1,0:T(8,128)S(1)}, f32[64,1024]{1,0:T(8,128)S(1)}, u32[]{:S(2)}, u32[]{:S(2)}) collective-permute-start(f32[64,1024]{1,0:T(8,128)S(1)} %fusion.180), channel_id=1, source_target_pairs={{0,4},{4,8},{8,12},{12,16},{16,20},{20,24},{24,28},{1,5},{5,9},{9,... | collective-permute-start | bytes 786440 | tf_op jit(solution)/shard_map/ppermute | solution.py:13
  135.1 42.1 %collective-permute-start.16 = (f32[64,1024]{1,0:T(8,128)S(1)}, f32[64,1024]{1,0:T(8,128)S(1)}, u32[]{:S(2)}, u32[]{:S(2)}) collective-permute-start(f32[64,1024]{1,0:T(8,128)S(1)} %fusion.177), channel_id=1, source_target_pairs={{0,16},{4,20},{8,24},{12,28},{1,17},{5,21},{9,25},{13,29},{2,18},{... | collective-permute-start | bytes 786440 | tf_op jit(solution)/shard_map/ppermute | solution.py:13
  150.9 26.4 %collective-permute-start.9 = (f32[64,1024]{1,0:T(8,128)S(1)}, f32[64,1024]{1,0:T(8,128)S(1)}, u32[]{:S(2)}, u32[]{:S(2)}) collective-permute-start(f32[64,1024]{1,0:T(8,128)S(1)} %fusion.177), channel_id=1, source_target_pairs={{0,4},{4,8},{8,12},{12,16},{16,20},{20,24},{24,28},{1,5},{5,9},{9,... | collective-permute-start | bytes 786440 | tf_op jit(solution)/shard_map/ppermute | solution.py:13
  182.6 5.1 %collective-permute-start.10 = (f32[64,1024]{1,0:T(8,128)S(1)}, f32[64,1024]{1,0:T(8,128)S(1)}, u32[]{:S(2)}, u32[]{:S(2)}) collective-permute-start(f32[64,1024]{1,0:T(8,128)S(1)} %fusion.201), channel_id=1, source_target_pairs={{0,4},{4,8},{8,12},{12,16},{16,20},{20,24},{24,28},{1,5},{5,9},{9,... | collective-permute-start | bytes 786440 | tf_op jit(solution)/shard_map/ppermute | solution.py:13
  185.0 10.0 %collective-permute-start.11 = (f32[64,1024]{1,0:T(8,128)S(1)}, f32[64,1024]{1,0:T(8,128)S(1)}, u32[]{:S(2)}, u32[]{:S(2)}) collective-permute-start(f32[64,1024]{1,0:T(8,128)S(1)} %fusion.201), channel_id=1, source_target_pairs={{0,16},{4,20},{8,24},{12,28},{1,17},{5,21},{9,25},{13,29},{2,18},{... | collective-permute-start | bytes 786440 | tf_op jit(solution)/shard_map/ppermute | solution.py:13
  205.6 19.6 %copy-start.1 = (f32[64,1024]{1,0:T(8,128)}, f32[64,1024]{1,0:T(8,128)S(1)}, u32[]{:S(2)}) copy-start(f32[64,1024]{1,0:T(8,128)S(1)} %fusion.210) | copy-start | bytes 786436
  205.6 12.5 %collective-permute-start.12 = (f32[64,1024]{1,0:T(8,128)S(1)}, f32[64,1024]{1,0:T(8,128)S(1)}, u32[]{:S(2)}, u32[]{:S(2)}) collective-permute-start(f32[64,1024]{1,0:T(8,128)S(1)} %fusion.210), channel_id=1, source_target_pairs={{0,4},{4,8},{8,12},{12,16},{16,20},{20,24},{24,28},{1,5},{5,9},{9,... | collective-permute-start | bytes 786440 | tf_op jit(solution)/shard_map/ppermute | solution.py:13
  207.5 12.3 %collective-permute-start.13 = (f32[64,1024]{1,0:T(8,128)S(1)}, f32[64,1024]{1,0:T(8,128)S(1)}, u32[]{:S(2)}, u32[]{:S(2)}) collective-permute-start(f32[64,1024]{1,0:T(8,128)S(1)} %fusion.210), channel_id=1, source_target_pairs={{0,16},{4,20},{8,24},{12,28},{1,17},{5,21},{9,25},{13,29},{2,18},{... | collective-permute-start | bytes 786440 | tf_op jit(solution)/shard_map/ppermute | solution.py:13
  230.4 12.9 %collective-permute-start.15 = (f32[64,1024]{1,0:T(8,128)S(1)}, f32[64,1024]{1,0:T(8,128)S(1)}, u32[]{:S(2)}, u32[]{:S(2)}) collective-permute-start(f32[64,1024]{1,0:T(8,128)S(1)} %fusion.219), channel_id=1, source_target_pairs={{0,16},{4,20},{8,24},{12,28},{1,17},{5,21},{9,25},{13,29},{2,18},{... | collective-permute-start | bytes 786440 | tf_op jit(solution)/shard_map/ppermute | solution.py:13
  234.8 4.8 %collective-permute-start.14 = (f32[64,1024]{1,0:T(8,128)S(1)}, f32[64,1024]{1,0:T(8,128)S(1)}, u32[]{:S(2)}, u32[]{:S(2)}) collective-permute-start(f32[64,1024]{1,0:T(8,128)S(1)} %fusion.219), channel_id=1, source_target_pairs={{0,4},{4,8},{8,12},{12,16},{16,20},{20,24},{24,28},{1,5},{5,9},{9,... | collective-permute-start | bytes 786440 | tf_op jit(solution)/shard_map/ppermute | solution.py:13
